TPU v7x, 32 devices: a whole 2x2x4 slice. The times are simulated.
32 devices in a mesh: heads: 2 (over x), seq: 16 (over z, y, core).
Axes of the slice: x: 2, y: 2, z: 4, core: 2. Of those that a mesh axis runs over, the one named last changes fastest.
Arguments:
- query_nope: bfloat16 [1, 4, 128, 128], P(None, None, 'heads'), may hold values from -6 to 6
- query_rope: bfloat16 [1, 4, 128, 64], P(None, None, 'heads'), may hold values from -8 to 8
- latent_cache: bfloat16 [1, 8192, 512], P(None, 'seq'), may hold values from -6 to 6
- rope_keys: bfloat16 [1, 64, 8192], P(None, None, 'seq'), may hold values from -8 to 8
- lengths: int32 [1], replicated, may hold values from 2 to 8189, as said below
- key_quant: bfloat16 [128, 512, 128], P('heads', 'seq'), may hold values from -127 to 127, as said below
- key_scale: float32 [128, 4], P('heads'), may hold values from 0.0006 to 0.0024
- value_quant: bfloat16 [128, 512, 128], P('heads', 'seq'), may hold values from -127 to 127, as said below
- value_scale: float32 [128, 4], P('heads'), may hold values from 0.0003 to 0.0012
- out_weight: bfloat16 [16384, 7168], P('heads', 'seq'), may hold values from -0.375 to 0.375
Outputs:
- attn_out: bfloat16 [1, 4, 7168], P(None, None, 'seq')
Inputs may be any that keep to these rules, and one draw needn't show every extreme that they name: `key_quant`: whole numbers. `value_quant`: whole numbers. `lengths`: one sequence has the largest allowed length, so that its last draft token sees all 8192 positions.
All inputs are finite; a program needn't handle non-finite values.
Results may differ from a plain program's by a relative error of at most 0.019.
Values may be sent and summed in bfloat16 or wider, within the bound.
A program may use at most 64 MiB of HBM per device.

v0:
```python
import jax
import jax.numpy as jnp
from jax import lax
from jax.sharding import PartitionSpec as P

QB = 128
neg_large = -1e30


def expand_scales(block_scale, offset, count):
    row_ids = (offset + jnp.arange(count, dtype=jnp.int32)) // QB
    onehot = (
        row_ids[:, None] == jnp.arange(block_scale.shape[1], dtype=jnp.int32)[None, :]
    ).astype(block_scale.dtype)
    return jnp.sum(block_scale[:, None, :] * onehot[None, :, :], axis=2)


def dequantize(quantized, block_scale, offset):
    factors = expand_scales(block_scale, offset, quantized.shape[1])
    return (quantized.astype(jnp.float32) * factors[:, :, None]).astype(jnp.bfloat16)


def per_device(
    query_nope,
    query_rope,
    latent_cache,
    rope_keys,
    lengths,
    key_quant,
    key_scale,
    value_quant,
    value_scale,
    out_weight,
):
    seq_index = lax.axis_index("seq")
    latent_cols = key_quant.shape[1]
    offset = seq_index * latent_cols
    factor = (query_nope.shape[-1] + query_rope.shape[-1]) ** (-0.5)
    key_weight = dequantize(key_quant, key_scale, offset)
    piece_lat = jnp.einsum(
        "btkn,kcn->btkc", query_nope, key_weight, preferred_element_type=jnp.float32
    ).astype(jnp.bfloat16)
    query_latent = lax.all_gather(piece_lat, "seq", axis=3, tiled=True)
    positions = latent_cache.shape[1]
    scores = jnp.einsum(
        "btkc,bsc->btks", query_latent, latent_cache, preferred_element_type=jnp.float32
    )
    scores = (
        scores
        + jnp.einsum("btkr,brs->btks", query_rope, rope_keys, preferred_element_type=jnp.float32)
    ) * factor
    position = seq_index * positions + jnp.arange(positions, dtype=jnp.int32)
    horizon = lengths[:, None] + jnp.arange(query_nope.shape[1], dtype=jnp.int32)[None, :]
    visible = (position[None, None, :] < horizon[:, :, None])[:, :, None, :]
    block_max = jnp.max(jnp.where(visible, scores, neg_large), axis=3)
    probs = jnp.where(visible, jnp.exp(scores - block_max[..., None]), 0.0)
    block_sum = jnp.sum(probs, axis=3)
    probs_bf = probs.astype(jnp.bfloat16)
    block_out = jnp.einsum(
        "btks,bsc->btkc", probs_bf, latent_cache, preferred_element_type=jnp.float32
    )
    top = lax.pmax(block_max, "seq")
    rescale = jnp.exp(block_max - top)
    totals = lax.psum(block_sum * rescale, "seq")
    shrink = jnp.exp(block_max - top)
    merged_slice = lax.psum_scatter(
        block_out * shrink[..., None], "seq", scatter_dimension=3, tiled=True
    )
    latent_slice = (merged_slice / totals[..., None]).astype(jnp.bfloat16)
    value_weight = dequantize(value_quant, value_scale, offset)
    partial_heads = jnp.einsum(
        "btkc,kcv->btkv", latent_slice, value_weight, preferred_element_type=jnp.float32
    )
    flat_terms = partial_heads.reshape(-1)
    share_sum = lax.psum_scatter(flat_terms, "seq", scatter_dimension=0, tiled=True).astype(
        jnp.bfloat16
    )
    head_output = lax.all_gather(share_sum, "seq", axis=0, tiled=True).reshape(partial_heads.shape)
    batch, drafts, heads_here, value_width = head_output.shape
    projected = jnp.dot(
        head_output.reshape(batch * drafts, heads_here * value_width),
        out_weight,
        preferred_element_type=jnp.float32,
    )
    summed = lax.psum(projected, "heads")
    return summed.astype(jnp.bfloat16).reshape(batch, drafts, out_weight.shape[1])


def solution(mesh):
    in_specs = (
        P(None, None, "heads", None),
        P(None, None, "heads", None),
        P(None, "seq", None),
        P(None, None, "seq"),
        P(),
        P("heads", "seq", None),
        P("heads", None),
        P("heads", "seq", None),
        P("heads", None),
        P("heads", "seq"),
    )
    out_specs = P(None, None, "seq")
    return jax.shard_map(
        per_device, mesh=mesh, in_specs=in_specs, out_specs=out_specs, check_vma=False
    )
```

profile of v0, /device:TPU:0, one launch (start us, length us, event | category | flops | bytes accessed | tf_op | source)
XLA Modules:
  0.0 255.0 jit_solution(11461911653005468374)
XLA Ops:
  7.3 0.8 multiply_reduce_fusion.1
  8.1 0.1 copy.31
  8.2 1.5 fusion.2
  9.7 0.1 copy.33
  9.8 24.6 %all_gather.6 = bf16[1,4,64,512]{2,1,0,3:T(4,128)(2,1)S(1)} all-gather(bf16[1,4,64,32]{2,1,0,3:T(4,128)(2,1)S(1)} %copy.33), channel_id=1, replica_groups=mesh['heads'=2,'seq'=16] {'seq'}, dimensions={3}, use_global_device_ids=true | all-gather | bytes 278528 | tf_op jit(solution)/shard_map/all_gather | solution.py:43
  34.4 0.3 copy.34
  34.7 0.1 broadcast_compare_fusion
  34.8 0.3 fusion.4
  35.2 1.2 select_reduce_fusion
  36.3 29.8 %pmax.7 = f32[1,4,64]{2,1,0:T(4,128)S(1)} all-reduce(f32[1,4,64]{2,1,0:T(4,128)S(1)} %bitcast.55), channel_id=1, replica_groups=mesh['heads'=2,'seq'=16] {'seq'}, use_global_device_ids=true, to_apply=%region_3.4 | all-reduce | flops 256 | bytes 2048 | tf_op jit(solution)/shard_map/pmax | solution.py:62
  66.2 0.2 fusion.8
  66.4 0.4 fusion.1
  66.8 1.4 copy.35
  68.2 0.6 dynamic-slice
  69.4 0.1 copy.30
  70.2 29.5 %psum.14 = f32[4,64]{1,0:T(4,128)S(1)} all-reduce(f32[4,64]{1,0:T(4,128)S(1)} %get-tuple-element.8), channel_id=1, replica_groups=mesh['heads'=2,'seq'=16] {'seq'}, use_global_device_ids=true, to_apply=%region_6.7 | all-reduce | flops 256 | bytes 2048 | tf_op jit(solution)/shard_map/psum | solution.py:64
  99.7 59.7 %all-reduce.5.cloned.1.call-done = f32[1,4,64,512]{2,1,0,3:T(4,128)} async-done(((f32[1,4,64,512]{2,1,0,3:T(4,128)}), f32[1,4,64,512]{2,1,0,3:T(4,128)}) %all-reduce.5.cloned.1.call-update) | async-done | bytes 524304
  159.4 0.9 fusion.19
  160.2 0.1 copy.36
  160.4 0.4 convolution_bitcast_fusion
  160.8 59.3 %all-reduce.6 = bf16[32768]{0:T(1024)(128)(2,1)S(1)} all-reduce(f32[32768]{0:T(1024)S(1)} %bitcast.54), channel_id=3, replica_groups=mesh['heads'=2,'seq'=16] {'seq'}, use_global_device_ids=true, to_apply=%region_7.8.clone | all-reduce | flops 32768 | bytes 196608
  220.1 17.3 %all_gather.7 = bf16[32768]{0:T(1024)(128)(2,1)S(1)} all-gather(bf16[2048]{0:T(1024)(128)(2,1)S(1)} %dynamic-slice.10), channel_id=1, replica_groups=mesh['heads'=2,'seq'=16] {'seq'}, dimensions={0}, use_global_device_ids=true | all-gather | bytes 69632 | tf_op jit(solution)/shard_map/all_gather | solution.py:78
  237.5 5.1 %fusion.24 = f32[4,448]{1,0:T(4,128)S(1)} fusion(bf16[4,8192]{1,0:T(4,128)(2,1)S(1)} %reshape_reshape.3, bf16[8192,448]{0,1:T(8,128)(2,1)} %param.19), kind=kOutput, calls=%fused_computation.46 | convolution fusion | flops 29360128 | bytes 7412736 | tf_op jit(solution)/shard_map/dot_general | solution.py:80
  242.5 5.6 %psum.15 = bf16[4,448]{1,0:T(4,128)(2,1)} all-reduce(f32[4,448]{1,0:T(4,128)S(1)} %fusion.24), channel_id=1, replica_groups=mesh['heads'=2,'seq'=16] {'heads'}, use_global_device_ids=true, to_apply=%region_8.9 | all-reduce | flops 1792 | bytes 10752 | tf_op jit(solution)/shard_map/psum | solution.py:85
  (16 shorter events, 0.1 us)
Async XLA Ops:
  6.5 28.3 %copy-start = (bf16[1,512,512]{2,1,0:T(8,128)(2,1)S(1)}, bf16[1,512,512]{2,1,0:T(8,128)(2,1)}, u32[]{:S(2)}) copy-start(bf16[1,512,512]{2,1,0:T(8,128)(2,1)} %param.12) | copy-start | bytes 1572868
  6.5 61.6 %copy-start.2 = (u32[32]{0:T(128)S(1)}, u32[32]{0:T(128)}, u32[]{:S(2)}) copy-start(u32[32]{0:T(128)} %constant.36) | copy-start | bytes 388
  6.5 153.8 %copy-start.1 = (bf16[64,32,128]{2,1,0:T(8,128)(2,1)S(1)}, bf16[64,32,128]{2,1,0:T(8,128)(2,1)}, u32[]{:S(2)}) copy-start(bf16[64,32,128]{2,1,0:T(8,128)(2,1)} %param.17) | copy-start | bytes 1572868
  6.5 152.8 %all-reduce.5.cloned.1.call-start = ((), (), s32[]{:S(2)}) async-start(), calls=%async_computation | async-start | bytes 2097152
Sparse Core Ops, SparseCore 0:
  68.3 91.0 all-reduce.4
where the time goes:
time: 255 us
  blocking collectives  166 us (65%)
  waiting for transfers between devices  59.7 us (23%)
  between operations  15.6 us (6%)
  matrix products  8.86 us (3%)
  local copies, waits for them, and re-layouts  2.7 us (1%)
    unnamed x2, waiting for transfers between devices  59.7 us
    unnamed x1, blocking collectives  59.3 us
    pmax x1, blocking collectives, per_device(): top = lax.pmax(block_max, 'seq')  29.8 us
    psum x1, blocking collectives, per_device(): totals = lax.psum(block_sum * rescale, 'seq')  29.5 us
    all_gather x1, blocking collectives, per_device(): query_latent = lax.all_gather(piece_lat, 'seq', axis=3, tiled=True)  24.6 us
    all_gather x1, blocking collectives, per_device(): lax.all_gather(share_sum, 'seq', axis=0, tiled=True)  17.3 us
    psum x1, blocking collectives, per_device(): summed = lax.psum(projected, 'heads')  5.57 us
  transfers between devices with their start and end apart: 1, of which 1 were waited for; matrix products, arithmetic and copies ran while one was open for 0% of the time, Pallas kernels for 0%

commit v1 on v0

--- a/solution.py
+++ b/solution.py
@@ -2,6 +2,7 @@
 import jax.numpy as jnp
 from jax import lax
 from jax.sharding import PartitionSpec as P
+from jax.lax import axis_index, axis_size, ppermute
 
 QB = 128
 neg_large = -1e30
@@ -40,10 +41,28 @@
     piece_lat = jnp.einsum(
         "btkn,kcn->btkc", query_nope, key_weight, preferred_element_type=jnp.float32
     ).astype(jnp.bfloat16)
-    query_latent = lax.all_gather(piece_lat, "seq", axis=3, tiled=True)
     positions = latent_cache.shape[1]
-    scores = jnp.einsum(
-        "btkc,bsc->btks", query_latent, latent_cache, preferred_element_type=jnp.float32
+
+    def write_core(block_here, mesh_name, sheet):
+        all_rows, inter = (axis_size(mesh_name), axis_index(mesh_name))
+        a_now = block_here.shape[3]
+        buffer = tuple(((dev, (dev - 1) % all_rows) for dev in range(all_rows)))
+        after = block_here
+        latest = sheet(after, inter * a_now)
+        for hop_no in range(1, all_rows):
+            after = ppermute(after, axis_name=mesh_name, perm=buffer)
+            latest = latest + sheet(after, (inter + hop_no) % all_rows * a_now)
+        return latest
+
+    scores = write_core(
+        piece_lat,
+        "seq",
+        lambda own_block, start: jnp.einsum(
+            "btkc,bsc->btks",
+            own_block,
+            lax.dynamic_slice_in_dim(latent_cache, start, own_block.shape[3], axis=2),
+            preferred_element_type=jnp.float32,
+        ),
     )
     scores = (
         scores

time: 255 us -> 330 us (1.29)
  starting transfers between devices: 0.01 us -> 67.8 us
  waiting for transfers between devices: 59.7 us -> 81.9 us
  blocking collectives: 166 us -> 146 us
  matrix products: 8.86 us -> 13.5 us
    ppermute x0 -> x15, starting transfers between devices: none -> 67.8 us  [write_core(): after = ppermute(after, axis_name=mesh_name, perm=buffer)]
    all_gather x1 -> x0, blocking collectives: 24.6 us -> none  [per_device(): query_latent = lax.all_gather(piece_lat, 'seq', axis=3, tiled=True)]
    ppermute x0 -> x15, waiting for transfers between devices: none -> 22.3 us  [write_core(): after = ppermute(after, axis_name=mesh_name, perm=buffer)]
    dot_general x1 -> x16, matrix products: 0.33 us -> 5.06 us  [per_device(): jnp.einsum('btkc,bsc->btks', own_block, lax.dynamic_slice_in_dim(latent_c...]
    pmax x1, blocking collectives: 29.8 us -> 34 us  [per_device(): top = lax.pmax(block_max, 'seq')]
  transfers between devices with their start and end apart: 1 -> 16, of which waited for: 1 -> 15; matrix products, arithmetic and copies ran while one was open for 0% -> 2% of each run, Pallas kernels for 0% -> 0%
where the time goes in v1:
time: 330 us; the launch traced here: 329 us
  blocking collectives  146 us (44%)
  waiting for transfers between devices  81.9 us (25%)
  starting transfers between devices  67.8 us (21%)
  between operations  15.7 us (5%)
  matrix products  13.5 us (4%)
    ppermute x15, starting transfers between devices, write_core(): after = ppermute(after, axis_name=mesh_name, perm=buffer)  67.8 us
    unnamed x2, waiting for transfers between devices  59.6 us
    unnamed x1, blocking collectives  59.3 us
    pmax x1, blocking collectives, per_device(): top = lax.pmax(block_max, 'seq')  34 us
    psum x1, blocking collectives, per_device(): totals = lax.psum(block_sum * rescale, 'seq')  29.8 us
    ppermute x15, waiting for transfers between devices, write_core(): after = ppermute(after, axis_name=mesh_name, perm=buffer)  22.3 us
    all_gather x1, blocking collectives, per_device(): lax.all_gather(share_sum, 'seq', axis=0, tiled=True)  17.3 us
  transfers between devices with their start and end apart: 16, of which 15 were waited for; matrix products, arithmetic and copies ran while one was open for 2% of the time, Pallas kernels for 0%

profile of v1, /device:TPU:0, one launch (start us, length us, event | category | flops | bytes accessed | tf_op | source)
XLA Modules:
  0.0 329.2 jit_solution(9395806502377732683)
XLA Ops:
  9.0 5.5 %collective-permute-start = (bf16[1,4,64,32]{3,1,2,0:T(4,128)(2,1)S(1)}, bf16[1,4,64,32]{3,1,2,0:T(4,128)(2,1)S(1)}, u32[]{:S(2)}, u32[]{:S(2)}) collective-permute-start(bf16[1,4,64,32]{3,1,2,0:T(4,128)(2,1)S(1)} %bitcast.145), channel_id=1, source_target_pairs={{0,15},{1,0},{2,1},{3,2},{4,3},{5,4},{6,5},{7,6},{8,7},{9,8},{10,9... | collective-permute-start | bytes 49160 | tf_op jit(solution)/shard_map/ppermute | solution.py:53
  16.8 4.1 %collective-permute-start.1 = (bf16[1,4,64,32]{3,1,2,0:T(4,128)(2,1)S(1)}, bf16[1,4,64,32]{3,1,2,0:T(4,128)(2,1)S(1)}, u32[]{:S(2)}, u32[]{:S(2)}) collective-permute-start(bf16[1,4,64,32]{3,1,2,0:T(4,128)(2,1)S(1)} %collective-permute-done), channel_id=1, source_target_pairs={{0,15},{1,0},{2,1},{3,2},{4,3},{5,4},{6,5},{7,6},{8,7},{9,8},{10,9... | collective-permute-start | bytes 49160 | tf_op jit(solution)/shard_map/ppermute | solution.py:53
  22.8 4.5 %collective-permute-start.2 = (bf16[1,4,64,32]{3,1,2,0:T(4,128)(2,1)S(1)}, bf16[1,4,64,32]{3,1,2,0:T(4,128)(2,1)S(1)}, u32[]{:S(2)}, u32[]{:S(2)}) collective-permute-start(bf16[1,4,64,32]{3,1,2,0:T(4,128)(2,1)S(1)} %collective-permute-done.1), channel_id=1, source_target_pairs={{0,15},{1,0},{2,1},{3,2},{4,3},{5,4},{6,5},{7,6},{8,7},{9,8},{10,9... | collective-permute-start | bytes 49160 | tf_op jit(solution)/shard_map/ppermute | solution.py:53
  27.6 1.6 collective-permute-done.2
  29.2 4.5 %collective-permute-start.3 = (bf16[1,4,64,32]{3,1,2,0:T(4,128)(2,1)S(1)}, bf16[1,4,64,32]{3,1,2,0:T(4,128)(2,1)S(1)}, u32[]{:S(2)}, u32[]{:S(2)}) collective-permute-start(bf16[1,4,64,32]{3,1,2,0:T(4,128)(2,1)S(1)} %collective-permute-done.2), channel_id=1, source_target_pairs={{0,15},{1,0},{2,1},{3,2},{4,3},{5,4},{6,5},{7,6},{8,7},{9,8},{10,9... | collective-permute-start | bytes 49160 | tf_op jit(solution)/shard_map/ppermute | solution.py:53
  35.6 4.5 %collective-permute-start.4 = (bf16[1,4,64,32]{3,1,2,0:T(4,128)(2,1)S(1)}, bf16[1,4,64,32]{3,1,2,0:T(4,128)(2,1)S(1)}, u32[]{:S(2)}, u32[]{:S(2)}) collective-permute-start(bf16[1,4,64,32]{3,1,2,0:T(4,128)(2,1)S(1)} %collective-permute-done.3), channel_id=1, source_target_pairs={{0,15},{1,0},{2,1},{3,2},{4,3},{5,4},{6,5},{7,6},{8,7},{9,8},{10,9... | collective-permute-start | bytes 49160 | tf_op jit(solution)/shard_map/ppermute | solution.py:53
  42.0 4.5 %collective-permute-start.5 = (bf16[1,4,64,32]{3,1,2,0:T(4,128)(2,1)S(1)}, bf16[1,4,64,32]{3,1,2,0:T(4,128)(2,1)S(1)}, u32[]{:S(2)}, u32[]{:S(2)}) collective-permute-start(bf16[1,4,64,32]{3,1,2,0:T(4,128)(2,1)S(1)} %collective-permute-done.4), channel_id=1, source_target_pairs={{0,15},{1,0},{2,1},{3,2},{4,3},{5,4},{6,5},{7,6},{8,7},{9,8},{10,9... | collective-permute-start | bytes 49160 | tf_op jit(solution)/shard_map/ppermute | solution.py:53
  48.4 4.5 %collective-permute-start.6 = (bf16[1,4,64,32]{3,1,2,0:T(4,128)(2,1)S(1)}, bf16[1,4,64,32]{3,1,2,0:T(4,128)(2,1)S(1)}, u32[]{:S(2)}, u32[]{:S(2)}) collective-permute-start(bf16[1,4,64,32]{3,1,2,0:T(4,128)(2,1)S(1)} %collective-permute-done.5), channel_id=1, source_target_pairs={{0,15},{1,0},{2,1},{3,2},{4,3},{5,4},{6,5},{7,6},{8,7},{9,8},{10,9... | collective-permute-start | bytes 49160 | tf_op jit(solution)/shard_map/ppermute | solution.py:53
  54.7 4.5 %collective-permute-start.7 = (bf16[1,4,64,32]{3,1,2,0:T(4,128)(2,1)S(1)}, bf16[1,4,64,32]{3,1,2,0:T(4,128)(2,1)S(1)}, u32[]{:S(2)}, u32[]{:S(2)}) collective-permute-start(bf16[1,4,64,32]{3,1,2,0:T(4,128)(2,1)S(1)} %collective-permute-done.6), channel_id=1, source_target_pairs={{0,15},{1,0},{2,1},{3,2},{4,3},{5,4},{6,5},{7,6},{8,7},{9,8},{10,9... | collective-permute-start | bytes 49160 | tf_op jit(solution)/shard_map/ppermute | solution.py:53
  61.1 4.5 %collective-permute-start.8 = (bf16[1,4,64,32]{3,1,2,0:T(4,128)(2,1)S(1)}, bf16[1,4,64,32]{3,1,2,0:T(4,128)(2,1)S(1)}, u32[]{:S(2)}, u32[]{:S(2)}) collective-permute-start(bf16[1,4,64,32]{3,1,2,0:T(4,128)(2,1)S(1)} %collective-permute-done.7), channel_id=1, source_target_pairs={{0,15},{1,0},{2,1},{3,2},{4,3},{5,4},{6,5},{7,6},{8,7},{9,8},{10,9... | collective-permute-start | bytes 49160 | tf_op jit(solution)/shard_map/ppermute | solution.py:53
  67.5 4.5 %collective-permute-start.9 = (bf16[1,4,64,32]{3,1,2,0:T(4,128)(2,1)S(1)}, bf16[1,4,64,32]{3,1,2,0:T(4,128)(2,1)S(1)}, u32[]{:S(2)}, u32[]{:S(2)}) collective-permute-start(bf16[1,4,64,32]{3,1,2,0:T(4,128)(2,1)S(1)} %collective-permute-done.8), channel_id=1, source_target_pairs={{0,15},{1,0},{2,1},{3,2},{4,3},{5,4},{6,5},{7,6},{8,7},{9,8},{10,9... | collective-permute-start | bytes 49160 | tf_op jit(solution)/shard_map/ppermute | solution.py:53
  73.9 4.5 %collective-permute-start.10 = (bf16[1,4,64,32]{3,1,2,0:T(4,128)(2,1)S(1)}, bf16[1,4,64,32]{3,1,2,0:T(4,128)(2,1)S(1)}, u32[]{:S(2)}, u32[]{:S(2)}) collective-permute-start(bf16[1,4,64,32]{3,1,2,0:T(4,128)(2,1)S(1)} %collective-permute-done.9), channel_id=1, source_target_pairs={{0,15},{1,0},{2,1},{3,2},{4,3},{5,4},{6,5},{7,6},{8,7},{9,8},{10,9... | collective-permute-start | bytes 49160 | tf_op jit(solution)/shard_map/ppermute | solution.py:53
  78.7 1.6 collective-permute-done.10
  80.3 4.5 %collective-permute-start.11 = (bf16[1,4,64,32]{3,1,2,0:T(4,128)(2,1)S(1)}, bf16[1,4,64,32]{3,1,2,0:T(4,128)(2,1)S(1)}, u32[]{:S(2)}, u32[]{:S(2)}) collective-permute-start(bf16[1,4,64,32]{3,1,2,0:T(4,128)(2,1)S(1)} %collective-permute-done.10), channel_id=1, source_target_pairs={{0,15},{1,0},{2,1},{3,2},{4,3},{5,4},{6,5},{7,6},{8,7},{9,8},{10,9... | collective-permute-start | bytes 49160 | tf_op jit(solution)/shard_map/ppermute | solution.py:53
  86.7 4.5 %collective-permute-start.12 = (bf16[1,4,64,32]{3,1,2,0:T(4,128)(2,1)S(1)}, bf16[1,4,64,32]{3,1,2,0:T(4,128)(2,1)S(1)}, u32[]{:S(2)}, u32[]{:S(2)}) collective-permute-start(bf16[1,4,64,32]{3,1,2,0:T(4,128)(2,1)S(1)} %collective-permute-done.11), channel_id=1, source_target_pairs={{0,15},{1,0},{2,1},{3,2},{4,3},{5,4},{6,5},{7,6},{8,7},{9,8},{10,9... | collective-permute-start | bytes 49160 | tf_op jit(solution)/shard_map/ppermute | solution.py:53
  93.1 4.5 %collective-permute-start.13 = (bf16[1,4,64,32]{3,1,2,0:T(4,128)(2,1)S(1)}, bf16[1,4,64,32]{3,1,2,0:T(4,128)(2,1)S(1)}, u32[]{:S(2)}, u32[]{:S(2)}) collective-permute-start(bf16[1,4,64,32]{3,1,2,0:T(4,128)(2,1)S(1)} %collective-permute-done.12), channel_id=1, source_target_pairs={{0,15},{1,0},{2,1},{3,2},{4,3},{5,4},{6,5},{7,6},{8,7},{9,8},{10,9... | collective-permute-start | bytes 49160 | tf_op jit(solution)/shard_map/ppermute | solution.py:53
  99.5 4.5 %collective-permute-start.14 = (bf16[1,4,64,32]{3,1,2,0:T(4,128)(2,1)S(1)}, bf16[1,4,64,32]{3,1,2,0:T(4,128)(2,1)S(1)}, u32[]{:S(2)}, u32[]{:S(2)}) collective-permute-start(bf16[1,4,64,32]{3,1,2,0:T(4,128)(2,1)S(1)} %collective-permute-done.13), channel_id=1, source_target_pairs={{0,15},{1,0},{2,1},{3,2},{4,3},{5,4},{6,5},{7,6},{8,7},{9,8},{10,9... | collective-permute-start | bytes 49160 | tf_op jit(solution)/shard_map/ppermute | solution.py:53
  106.3 34.0 %pmax.7 = f32[1,4,64]{2,1,0:T(4,128)S(1)} all-reduce(f32[1,4,64]{2,1,0:T(4,128)S(1)} %bitcast.161), channel_id=1, replica_groups=mesh['heads'=2,'seq'=16] {'seq'}, use_global_device_ids=true, to_apply=%region_3.4 | all-reduce | flops 256 | bytes 2048 | tf_op jit(solution)/shard_map/pmax | solution.py:81
  144.3 29.8 %psum.14 = f32[4,64]{1,0:T(4,128)S(1)} all-reduce(f32[4,64]{1,0:T(4,128)S(1)} %get-tuple-element.8), channel_id=1, replica_groups=mesh['heads'=2,'seq'=16] {'seq'}, use_global_device_ids=true, to_apply=%region_6.7 | all-reduce | flops 256 | bytes 2048 | tf_op jit(solution)/shard_map/psum | solution.py:83
  174.0 59.6 %all-reduce.5.cloned.1.call-done = f32[1,4,64,512]{2,1,0,3:T(4,128)} async-done(((f32[1,4,64,512]{2,1,0,3:T(4,128)}), f32[1,4,64,512]{2,1,0,3:T(4,128)}) %all-reduce.5.cloned.1.call-update) | async-done | bytes 524304
  235.1 59.3 %all-reduce.6 = bf16[32768]{0:T(1024)(128)(2,1)S(1)} all-reduce(f32[32768]{0:T(1024)S(1)} %bitcast.143), channel_id=3, replica_groups=mesh['heads'=2,'seq'=16] {'seq'}, use_global_device_ids=true, to_apply=%region_7.8.clone | all-reduce | flops 32768 | bytes 196608
  294.4 17.3 %all_gather.3 = bf16[32768]{0:T(1024)(128)(2,1)S(1)} all-gather(bf16[2048]{0:T(1024)(128)(2,1)S(1)} %dynamic-slice.10), channel_id=1, replica_groups=mesh['heads'=2,'seq'=16] {'seq'}, dimensions={0}, use_global_device_ids=true | all-gather | bytes 69632 | tf_op jit(solution)/shard_map/all_gather | solution.py:97
  311.7 5.1 %fusion.87 = f32[4,448]{1,0:T(4,128)S(1)} fusion(bf16[4,8192]{1,0:T(4,128)(2,1)S(1)} %reshape_reshape.3, bf16[8192,448]{0,1:T(8,128)(2,1)} %param.19), kind=kOutput, calls=%fused_computation.123 | convolution fusion | flops 29360128 | bytes 7412736 | tf_op jit(solution)/shard_map/dot_general | solution.py:99
  316.8 5.6 %psum.15 = bf16[4,448]{1,0:T(4,128)(2,1)} all-reduce(f32[4,448]{1,0:T(4,128)S(1)} %fusion.87), channel_id=1, replica_groups=mesh['heads'=2,'seq'=16] {'heads'}, use_global_device_ids=true, to_apply=%region_8.9 | all-reduce | flops 1792 | bytes 10752 | tf_op jit(solution)/shard_map/psum | solution.py:104
  (58 shorter events, 31.9 us)
Async XLA Ops:
  6.5 9.7 %copy-start = (bf16[1,512,512]{2,1,0:T(8,128)(2,1)S(1)}, bf16[1,512,512]{2,1,0:T(8,128)(2,1)}, u32[]{:S(2)}) copy-start(bf16[1,512,512]{2,1,0:T(8,128)(2,1)} %param.12) | copy-start | bytes 1572868
  6.5 227.1 %all-reduce.5.cloned.1.call-start = ((), (), s32[]{:S(2)}) async-start(), calls=%async_computation | async-start | bytes 2097152
  9.0 7.8 %collective-permute-start = (bf16[1,4,64,32]{3,1,2,0:T(4,128)(2,1)S(1)}, bf16[1,4,64,32]{3,1,2,0:T(4,128)(2,1)S(1)}, u32[]{:S(2)}, u32[]{:S(2)}) collective-permute-start(bf16[1,4,64,32]{3,1,2,0:T(4,128)(2,1)S(1)} %bitcast.145), channel_id=1, source_target_pairs={{0,15},{1,0},{2,1},{3,2},{4,3},{5,4},{6,5},{7,6},{8,7},{9,8},{10,9... | collective-permute-start | bytes 49160 | tf_op jit(solution)/shard_map/ppermute | solution.py:53
  16.8 6.0 %collective-permute-start.1 = (bf16[1,4,64,32]{3,1,2,0:T(4,128)(2,1)S(1)}, bf16[1,4,64,32]{3,1,2,0:T(4,128)(2,1)S(1)}, u32[]{:S(2)}, u32[]{:S(2)}) collective-permute-start(bf16[1,4,64,32]{3,1,2,0:T(4,128)(2,1)S(1)} %collective-permute-done), channel_id=1, source_target_pairs={{0,15},{1,0},{2,1},{3,2},{4,3},{5,4},{6,5},{7,6},{8,7},{9,8},{10,9... | collective-permute-start | bytes 49160 | tf_op jit(solution)/shard_map/ppermute | solution.py:53
  22.8 6.4 %collective-permute-start.2 = (bf16[1,4,64,32]{3,1,2,0:T(4,128)(2,1)S(1)}, bf16[1,4,64,32]{3,1,2,0:T(4,128)(2,1)S(1)}, u32[]{:S(2)}, u32[]{:S(2)}) collective-permute-start(bf16[1,4,64,32]{3,1,2,0:T(4,128)(2,1)S(1)} %collective-permute-done.1), channel_id=1, source_target_pairs={{0,15},{1,0},{2,1},{3,2},{4,3},{5,4},{6,5},{7,6},{8,7},{9,8},{10,9... | collective-permute-start | bytes 49160 | tf_op jit(solution)/shard_map/ppermute | solution.py:53
  29.2 6.4 %collective-permute-start.3 = (bf16[1,4,64,32]{3,1,2,0:T(4,128)(2,1)S(1)}, bf16[1,4,64,32]{3,1,2,0:T(4,128)(2,1)S(1)}, u32[]{:S(2)}, u32[]{:S(2)}) collective-permute-start(bf16[1,4,64,32]{3,1,2,0:T(4,128)(2,1)S(1)} %collective-permute-done.2), channel_id=1, source_target_pairs={{0,15},{1,0},{2,1},{3,2},{4,3},{5,4},{6,5},{7,6},{8,7},{9,8},{10,9... | collective-permute-start | bytes 49160 | tf_op jit(solution)/shard_map/ppermute | solution.py:53
  35.6 6.4 %collective-permute-start.4 = (bf16[1,4,64,32]{3,1,2,0:T(4,128)(2,1)S(1)}, bf16[1,4,64,32]{3,1,2,0:T(4,128)(2,1)S(1)}, u32[]{:S(2)}, u32[]{:S(2)}) collective-permute-start(bf16[1,4,64,32]{3,1,2,0:T(4,128)(2,1)S(1)} %collective-permute-done.3), channel_id=1, source_target_pairs={{0,15},{1,0},{2,1},{3,2},{4,3},{5,4},{6,5},{7,6},{8,7},{9,8},{10,9... | collective-permute-start | bytes 49160 | tf_op jit(solution)/shard_map/ppermute | solution.py:53
  42.0 6.4 %collective-permute-start.5 = (bf16[1,4,64,32]{3,1,2,0:T(4,128)(2,1)S(1)}, bf16[1,4,64,32]{3,1,2,0:T(4,128)(2,1)S(1)}, u32[]{:S(2)}, u32[]{:S(2)}) collective-permute-start(bf16[1,4,64,32]{3,1,2,0:T(4,128)(2,1)S(1)} %collective-permute-done.4), channel_id=1, source_target_pairs={{0,15},{1,0},{2,1},{3,2},{4,3},{5,4},{6,5},{7,6},{8,7},{9,8},{10,9... | collective-permute-start | bytes 49160 | tf_op jit(solution)/shard_map/ppermute | solution.py:53
  48.4 6.4 %collective-permute-start.6 = (bf16[1,4,64,32]{3,1,2,0:T(4,128)(2,1)S(1)}, bf16[1,4,64,32]{3,1,2,0:T(4,128)(2,1)S(1)}, u32[]{:S(2)}, u32[]{:S(2)}) collective-permute-start(bf16[1,4,64,32]{3,1,2,0:T(4,128)(2,1)S(1)} %collective-permute-done.5), channel_id=1, source_target_pairs={{0,15},{1,0},{2,1},{3,2},{4,3},{5,4},{6,5},{7,6},{8,7},{9,8},{10,9... | collective-permute-start | bytes 49160 | tf_op jit(solution)/shard_map/ppermute | solution.py:53
  54.7 6.4 %collective-permute-start.7 = (bf16[1,4,64,32]{3,1,2,0:T(4,128)(2,1)S(1)}, bf16[1,4,64,32]{3,1,2,0:T(4,128)(2,1)S(1)}, u32[]{:S(2)}, u32[]{:S(2)}) collective-permute-start(bf16[1,4,64,32]{3,1,2,0:T(4,128)(2,1)S(1)} %collective-permute-done.6), channel_id=1, source_target_pairs={{0,15},{1,0},{2,1},{3,2},{4,3},{5,4},{6,5},{7,6},{8,7},{9,8},{10,9... | collective-permute-start | bytes 49160 | tf_op jit(solution)/shard_map/ppermute | solution.py:53
  61.1 6.4 %collective-permute-start.8 = (bf16[1,4,64,32]{3,1,2,0:T(4,128)(2,1)S(1)}, bf16[1,4,64,32]{3,1,2,0:T(4,128)(2,1)S(1)}, u32[]{:S(2)}, u32[]{:S(2)}) collective-permute-start(bf16[1,4,64,32]{3,1,2,0:T(4,128)(2,1)S(1)} %collective-permute-done.7), channel_id=1, source_target_pairs={{0,15},{1,0},{2,1},{3,2},{4,3},{5,4},{6,5},{7,6},{8,7},{9,8},{10,9... | collective-permute-start | bytes 49160 | tf_op jit(solution)/shard_map/ppermute | solution.py:53
  65.6 76.6 %copy-start.2 = (u32[32]{0:T(128)S(1)}, u32[32]{0:T(128)}, u32[]{:S(2)}) copy-start(u32[32]{0:T(128)} %constant.132) | copy-start | bytes 388
  65.9 168.7 %copy-start.1 = (bf16[64,32,128]{2,1,0:T(8,128)(2,1)S(1)}, bf16[64,32,128]{2,1,0:T(8,128)(2,1)}, u32[]{:S(2)}) copy-start(bf16[64,32,128]{2,1,0:T(8,128)(2,1)} %param.17) | copy-start | bytes 1572868
  67.5 6.4 %collective-permute-start.9 = (bf16[1,4,64,32]{3,1,2,0:T(4,128)(2,1)S(1)}, bf16[1,4,64,32]{3,1,2,0:T(4,128)(2,1)S(1)}, u32[]{:S(2)}, u32[]{:S(2)}) collective-permute-start(bf16[1,4,64,32]{3,1,2,0:T(4,128)(2,1)S(1)} %collective-permute-done.8), channel_id=1, source_target_pairs={{0,15},{1,0},{2,1},{3,2},{4,3},{5,4},{6,5},{7,6},{8,7},{9,8},{10,9... | collective-permute-start | bytes 49160 | tf_op jit(solution)/shard_map/ppermute | solution.py:53
  73.9 6.4 %collective-permute-start.10 = (bf16[1,4,64,32]{3,1,2,0:T(4,128)(2,1)S(1)}, bf16[1,4,64,32]{3,1,2,0:T(4,128)(2,1)S(1)}, u32[]{:S(2)}, u32[]{:S(2)}) collective-permute-start(bf16[1,4,64,32]{3,1,2,0:T(4,128)(2,1)S(1)} %collective-permute-done.9), channel_id=1, source_target_pairs={{0,15},{1,0},{2,1},{3,2},{4,3},{5,4},{6,5},{7,6},{8,7},{9,8},{10,9... | collective-permute-start | bytes 49160 | tf_op jit(solution)/shard_map/ppermute | solution.py:53
  80.3 6.4 %collective-permute-start.11 = (bf16[1,4,64,32]{3,1,2,0:T(4,128)(2,1)S(1)}, bf16[1,4,64,32]{3,1,2,0:T(4,128)(2,1)S(1)}, u32[]{:S(2)}, u32[]{:S(2)}) collective-permute-start(bf16[1,4,64,32]{3,1,2,0:T(4,128)(2,1)S(1)} %collective-permute-done.10), channel_id=1, source_target_pairs={{0,15},{1,0},{2,1},{3,2},{4,3},{5,4},{6,5},{7,6},{8,7},{9,8},{10,9... | collective-permute-start | bytes 49160 | tf_op jit(solution)/shard_map/ppermute | solution.py:53
  86.7 6.4 %collective-permute-start.12 = (bf16[1,4,64,32]{3,1,2,0:T(4,128)(2,1)S(1)}, bf16[1,4,64,32]{3,1,2,0:T(4,128)(2,1)S(1)}, u32[]{:S(2)}, u32[]{:S(2)}) collective-permute-start(bf16[1,4,64,32]{3,1,2,0:T(4,128)(2,1)S(1)} %collective-permute-done.11), channel_id=1, source_target_pairs={{0,15},{1,0},{2,1},{3,2},{4,3},{5,4},{6,5},{7,6},{8,7},{9,8},{10,9... | collective-permute-start | bytes 49160 | tf_op jit(solution)/shard_map/ppermute | solution.py:53
  93.1 6.4 %collective-permute-start.13 = (bf16[1,4,64,32]{3,1,2,0:T(4,128)(2,1)S(1)}, bf16[1,4,64,32]{3,1,2,0:T(4,128)(2,1)S(1)}, u32[]{:S(2)}, u32[]{:S(2)}) collective-permute-start(bf16[1,4,64,32]{3,1,2,0:T(4,128)(2,1)S(1)} %collective-permute-done.12), channel_id=1, source_target_pairs={{0,15},{1,0},{2,1},{3,2},{4,3},{5,4},{6,5},{7,6},{8,7},{9,8},{10,9... | collective-permute-start | bytes 49160 | tf_op jit(solution)/shard_map/ppermute | solution.py:53
  99.5 6.4 %collective-permute-start.14 = (bf16[1,4,64,32]{3,1,2,0:T(4,128)(2,1)S(1)}, bf16[1,4,64,32]{3,1,2,0:T(4,128)(2,1)S(1)}, u32[]{:S(2)}, u32[]{:S(2)}) collective-permute-start(bf16[1,4,64,32]{3,1,2,0:T(4,128)(2,1)S(1)} %collective-permute-done.13), channel_id=1, source_target_pairs={{0,15},{1,0},{2,1},{3,2},{4,3},{5,4},{6,5},{7,6},{8,7},{9,8},{10,9... | collective-permute-start | bytes 49160 | tf_op jit(solution)/shard_map/ppermute | solution.py:53
Sparse Core Ops, SparseCore 0:
  142.4 91.2 all-reduce.4
